TPU v7x, 32 devices: a whole 2x2x4 slice. The times are simulated.
32 devices in a mesh: scan: 2 (over x), slab: 16 (over z, y, core).
Axes of the slice: x: 2, y: 2, z: 4, core: 2. Of those that a mesh axis runs over, the one named last changes fastest.
Arguments:
- kernels: bfloat16 [4, 6, 6, 6, 16384], P('scan', None, None, None, 'slab'), parts along dimension 0, may hold values from -0.013671875 to 0.013671875
Outputs:
- gram: float32 [4, 32, 1, 192, 1024], P('scan', 'slab'), parts along dimension 0
There are 2 independent parts, one for each index of `scan`. A program takes and returns all parts, laid end to end along the dimension named above; each array names one. Nothing has to cross between parts.
All inputs are finite; a program needn't handle non-finite values.
Results may differ from a plain program's by a relative error of at most 0.0023.
Values may be sent and summed in bfloat16 or wider, within the bound.
A program may use at most 128 MiB of HBM per device.

v0:
```python
import math

import jax
import jax.numpy as jnp
from jax import lax
from jax.sharding import PartitionSpec as P

COILS = 32
TAP = 6
NY = 256
NZ = 192
XD = 2
YW = 1
YLO = 127


full_turn = 2.0 * math.pi


def first_segment(columns, planes, length):
    shape = (planes.shape[0],) + columns.shape[2:]
    real_sum = jnp.zeros(shape, jnp.float32)
    imag_sum = jnp.zeros(shape, jnp.float32)
    for offset in range(columns.shape[1]):
        angle = (planes * offset % length).astype(jnp.float32) * (full_turn / length)
        cosine = jnp.cos(angle)[:, None, None, None]
        sine = jnp.sin(angle)[:, None, None, None]
        real_tap = columns[0, offset].astype(jnp.float32)[None]
        imag_tap = columns[1, offset].astype(jnp.float32)[None]
        real_sum = real_sum + real_tap * cosine - imag_tap * sine
        imag_sum = imag_sum + real_tap * sine + imag_tap * cosine
    return jnp.stack([real_sum, imag_sum]).astype(jnp.bfloat16)


def second_segment(first, rows, length):
    shape = (first.shape[1], rows.shape[0], first.shape[3], first.shape[4])
    real_sum = jnp.zeros(shape, jnp.float32)
    imag_sum = jnp.zeros(shape, jnp.float32)
    for offset in range(first.shape[2]):
        angle = (rows * offset % length).astype(jnp.float32) * (full_turn / length)
        cosine = jnp.cos(angle)[None, :, None, None]
        sine = jnp.sin(angle)[None, :, None, None]
        real_tap = first[0, :, offset].astype(jnp.float32)[:, None]
        imag_tap = first[1, :, offset].astype(jnp.float32)[:, None]
        real_sum = real_sum + real_tap * cosine - imag_tap * sine
        imag_sum = imag_sum + real_tap * sine + imag_tap * cosine
    return jnp.stack([real_sum, imag_sum], axis=2).astype(jnp.bfloat16)


def depth_table(length, taps):
    depth = jnp.arange(length, dtype=jnp.int32)
    offsets = jnp.arange(taps, dtype=jnp.int32)
    angle = (depth[:, None] * offsets[None, :] % length).astype(jnp.float32) * (full_turn / length)
    cosine = jnp.cos(angle)
    sine = jnp.sin(angle)
    table = jnp.stack(
        [jnp.stack([cosine, -sine], axis=1), jnp.stack([sine, cosine], axis=1)], axis=1
    )
    return table.reshape(length * 2, 2 * taps).astype(jnp.bfloat16)


def local(kernels):
    slab_count = lax.axis_size("slab")
    plane_total = XD * slab_count
    rows = YLO + jnp.arange(YW, dtype=jnp.int32)
    every_plane = jnp.arange(plane_total, dtype=jnp.int32)
    local_window = second_segment(first_segment(kernels, every_plane, plane_total), rows, NY)
    second = lax.all_to_all(local_window, "slab", split_axis=0, concat_axis=4, tiled=True)
    column_total = second.shape[4]
    blocks = second.reshape(XD * YW, 2 * TAP, column_total)
    table = depth_table(NZ, TAP)

    def one_block(block):
        images = jnp.dot(table, block, preferred_element_type=jnp.float32).astype(jnp.bfloat16)
        images = images.reshape(NZ, 2 * COILS, column_total // COILS)
        full = lax.dot_general(
            images, images, (((2,), (2,)), ((0,), (0,))), preferred_element_type=jnp.float32
        )
        full = full.reshape(NZ, 2, COILS, 2, COILS)
        real_part = full[:, 0, :, 0, :] + full[:, 1, :, 1, :]
        imag_part = full[:, 0, :, 1, :] - full[:, 1, :, 0, :]
        return jnp.stack([real_part, imag_part]).reshape(2, NZ, COILS * COILS)

    grams = lax.map(one_block, blocks)
    return jnp.moveaxis(grams, 1, 0).reshape(2, XD, YW, NZ, COILS * COILS)


def solution(mesh):
    return jax.shard_map(
        local,
        mesh=mesh,
        in_specs=(P("scan", None, None, None, "slab"),),
        out_specs=P("scan", "slab", None, None, None),
        check_vma=False,
    )
```

profile of v0, /device:TPU:29, one launch (start us, length us, event | category | flops | bytes accessed | tf_op | source)
XLA Modules:
  0.0 179.9 jit_solution(4888732102143296608)
XLA Ops:
  0.0 0.1 fusion.76
  0.1 0.1 fusion.78
  0.1 0.1 fusion.80
  0.2 0.1 fusion.82
  0.3 3.1 %fusion.86 = (bf16[1,1,6,6,1024]{4,0,3,2,1:T(2,128)(2,1)S(1)}, bf16[1,1,6,6,1024]{4,0,3,2,1:T(2,128)(2,1)S(1)}, bf16[1,1,6,6,1024]{4,0,3,2,1:T(2,128)(2,1)S(1)},...) fusion(bf16[2,6,6,6,1024]{4,0,3,2,1:T(2,128)(2,1)} %param.3), kind=kLoop, calls=%fused_computation.155 | loop fusion | bytes 1769472 | tf_op jit(solution)/shard_map/slice | solution.py:29
  3.4 0.1 fusion.48
  3.5 0.1 fusion.50
  3.6 0.1 fusion.52
  3.7 0.1 fusion.54
  3.7 0.1 fusion.56
  3.8 0.1 convert_add_fusion.1
  3.9 3.9 %add_convert_fusion = bf16[1,32,6,6,1024]{4,1,3,2,0:T(8,128)(2,1)S(1)} fusion(f32[6,6,1024]{2,1,0:T(8,128)S(1)} %get-tuple-element.66, f32[32]{0:T(128)S(1)} %get-tuple-element.80, f32[6,6,1024]{2,1,0:T(8,128)S(1)} %get-tuple-element.70, f32[32]{0:T(128)S(1)} %get-tuple-element.81, f32[6,6,1024]{2,1,0:T(8,128)S(1)} %get-tuple-element.71, ...), kind=kLoop, calls=%fused_computation.9 | loop fusion | flops 24772608 | bytes 3982592 | tf_op jit(solution)/shard_map/convert.27
  7.9 4.1 %subtract_convert_fusion = bf16[1,32,6,6,1024]{4,1,3,2,0:T(8,128)(2,1)S(1)} fusion(f32[32]{0:T(128)S(1)} %get-tuple-element.80, f32[6,6,1024]{2,1,0:T(8,128)S(1)} %get-tuple-element.70, f32[32]{0:T(128)S(1)} %get-tuple-element.81, f32[6,6,1024]{2,1,0:T(8,128)S(1)} %get-tuple-element.71, f32[32]{0:T(128)S(1)} %get-tuple-element.82, ...), kind=kLoop, calls=%fused_computation.10 | loop fusion | flops 24772608 | bytes 3982592 | tf_op jit(solution)/shard_map/convert.26
  12.0 1.1 fusion.47
  13.1 1.1 fusion.46
  14.2 0.1 pad_maximum_fusion.1
  14.3 1.7 copy.97
  16.0 6.3 %all-to-all-start = ((bf16[32,1,2,6,1024]{4,2,3,1,0:T(2,128)(2,1)}), bf16[32,1,2,6,1024]{4,2,3,1,0:T(2,128)(2,1)S(1)}, u32[]{:S(2)}, u32[]{:S(2)}) async-start(bf16[32,1,2,6,1024]{4,2,3,1,0:T(2,128)(2,1)} %copy.97), calls=%async_computation | async-start | bytes 1572864 | tf_op jit(solution)/shard_map/all_to_all | solution.py:68
  22.3 0.2 fusion.61
  22.5 0.2 negate_convert_fusion
  22.7 0.2 copy.99
  22.9 0.1 convert_element_type.675
  23.1 0.1 copy.101
  23.2 17.4 %all-to-all-done = bf16[32,1,2,6,1024]{4,2,3,1,0:T(2,128)(2,1)S(1)} async-done(((bf16[32,1,2,6,1024]{4,2,3,1,0:T(2,128)(2,1)}), bf16[32,1,2,6,1024]{4,2,3,1,0:T(2,128)(2,1)S(1)}, u32[]{:S(2)}, u32[]{:S(2)}) %all-to-all-start) | async-done | bytes 786464 | tf_op jit(solution)/shard_map/all_to_all | solution.py:68
  40.6 0.4 copy.103
  41.0 0.5 reshape.1088
  41.6 138.3 %while.10 = (s32[]{:T(128)}, f32[2,2,192,1024]{3,2,0,1:T(8,128)}, bf16[2,12,16384]{2,1,0:T(8,128)(2,1)S(1)}, bf16[384,12]{0,1:T(8,128)(2,1)S(1)}, s32[]{:T(128)}) while((s32[]{:T(128)}, f32[2,2,192,1024]{3,2,0,1:T(8,128)}, bf16[2,12,16384]{2,1,0:T(8,128)(2,1)S(1)}, bf16[384,12]{0,1:T(8,128)(2,1)S(1)}, s32[]{:T(128)}) %tuple.49), condition=%wide.region_1.2_spmd, body=%wide.region_0.1_spmd.sunk | while | flops 963379200 | bytes 99627584 | solution.py:84
  41.6 6.4 %fusion.101 = bf16[384,16384]{0,1:T(8,128)(2,1)} fusion(bf16[384,12]{0,1:T(8,128)(2,1)S(1)} %get-tuple-element.134, bf16[2,12,16384]{2,1,0:T(8,128)(2,1)S(1)} %get-tuple-element.133, s32[]{:T(128)} %get-tuple-element.126), kind=kOutput, calls=%fused_computation.1.clone.1 | convolution fusion | flops 157286400 | bytes 13119492 | tf_op jit(solution)/shard_map/while/body/eval_jaxpr/dot_general | solution.py:74
  48.0 16.7 %copy.162 = bf16[384,16384]{1,0:T(8,128)(2,1)} copy(bf16[384,16384]{0,1:T(8,128)(2,1)} %fusion.101) | data formatting | bytes 25165824 | tf_op jit(solution)/shard_map/while/body/eval_jaxpr/convert_element_type | solution.py:74
  64.6 19.6 %reshape.1090 = bf16[192,64,512]{2,1,0:T(8,128)(2,1)} reshape(bf16[384,16384]{1,0:T(8,128)(2,1)} %copy.162) | data formatting | bytes 25165824 | tf_op jit(solution)/shard_map/while/body/eval_jaxpr/reshape | solution.py:75
  84.2 12.6 %fusion.102 = f32[192,64,64]{2,1,0:T(8,128)} fusion(bf16[192,64,512]{2,1,0:T(8,128)(2,1)} %reshape.1090), kind=kOutput, calls=%fused_computation.156.clone.1 | convolution fusion | flops 805306368 | bytes 15728640 | tf_op jit(solution)/shard_map/while/body/eval_jaxpr/dot_general | solution.py:76
  96.9 6.7 %copy.163 = f32[192,64,64]{0,2,1:T(8,128)} copy(f32[192,64,64]{2,1,0:T(8,128)} %fusion.102) | data formatting | bytes 6291456 | tf_op jit(solution)/shard_map/while/body/eval_jaxpr/dot_general | solution.py:76
  103.6 2.6 %slice_add_fusion.2 = (f32[192,1,32,1,32]{0,4,3,2,1:T(8,128)S(1)}, f32[192,1,32,1,32]{0,4,3,2,1:T(8,128)S(1)}) fusion(f32[192,2,32,2,32]{0,4,3,2,1:T(8,128)} %bitcast.283), kind=kLoop, calls=%fused_computation.4.clone.1 | loop fusion | flops 393216 | bytes 4718592 | tf_op jit(solution)/shard_map/while/body/eval_jaxpr/add | solution.py:80
  106.2 0.1 pad_maximum_fusion.4
  106.3 1.7 copy.164
  108.1 2.7 %constant_dynamic-update-slice_fusion.2 = f32[2,2,192,1024]{3,2,0,1:T(8,128)} fusion(f32[2,2,192,1024]{3,2,0,1:T(8,128)} %get-tuple-element.127, f32[1,2,192,1024]{3,2,0,1:T(8,128)} %copy.164, s32[]{:T(128)} %get-tuple-element.126), kind=kLoop, calls=%fused_computation.7.clone.1 | loop fusion | bytes 3146240 | tf_op jit(solution)/shard_map/while/body/jit(dynamic_update_index_in_dim)/dynamic_update_slice | solution.py:84
  110.8 6.3 %fusion.101 = bf16[384,16384]{0,1:T(8,128)(2,1)} fusion(bf16[384,12]{0,1:T(8,128)(2,1)S(1)} %get-tuple-element.134, bf16[2,12,16384]{2,1,0:T(8,128)(2,1)S(1)} %get-tuple-element.133, s32[]{:T(128)} %get-tuple-element.126), kind=kOutput, calls=%fused_computation.1.clone.1 | convolution fusion | flops 157286400 | bytes 13119492 | tf_op jit(solution)/shard_map/while/body/eval_jaxpr/dot_general | solution.py:74
  117.1 16.7 %copy.162 = bf16[384,16384]{1,0:T(8,128)(2,1)} copy(bf16[384,16384]{0,1:T(8,128)(2,1)} %fusion.101) | data formatting | bytes 25165824 | tf_op jit(solution)/shard_map/while/body/eval_jaxpr/convert_element_type | solution.py:74
  133.8 19.6 %reshape.1090 = bf16[192,64,512]{2,1,0:T(8,128)(2,1)} reshape(bf16[384,16384]{1,0:T(8,128)(2,1)} %copy.162) | data formatting | bytes 25165824 | tf_op jit(solution)/shard_map/while/body/eval_jaxpr/reshape | solution.py:75
  153.4 12.6 %fusion.102 = f32[192,64,64]{2,1,0:T(8,128)} fusion(bf16[192,64,512]{2,1,0:T(8,128)(2,1)} %reshape.1090), kind=kOutput, calls=%fused_computation.156.clone.1 | convolution fusion | flops 805306368 | bytes 15728640 | tf_op jit(solution)/shard_map/while/body/eval_jaxpr/dot_general | solution.py:76
  166.0 6.7 %copy.163 = f32[192,64,64]{0,2,1:T(8,128)} copy(f32[192,64,64]{2,1,0:T(8,128)} %fusion.102) | data formatting | bytes 6291456 | tf_op jit(solution)/shard_map/while/body/eval_jaxpr/dot_general | solution.py:76
  172.7 2.6 %slice_add_fusion.2 = (f32[192,1,32,1,32]{0,4,3,2,1:T(8,128)S(1)}, f32[192,1,32,1,32]{0,4,3,2,1:T(8,128)S(1)}) fusion(f32[192,2,32,2,32]{0,4,3,2,1:T(8,128)} %bitcast.283), kind=kLoop, calls=%fused_computation.4.clone.1 | loop fusion | flops 393216 | bytes 4718592 | tf_op jit(solution)/shard_map/while/body/eval_jaxpr/add | solution.py:80
  175.3 0.1 pad_maximum_fusion.4
  175.5 1.7 copy.164
  177.2 2.7 %constant_dynamic-update-slice_fusion.2 = f32[2,2,192,1024]{3,2,0,1:T(8,128)} fusion(f32[2,2,192,1024]{3,2,0,1:T(8,128)} %get-tuple-element.127, f32[1,2,192,1024]{3,2,0,1:T(8,128)} %copy.164, s32[]{:T(128)} %get-tuple-element.126), kind=kLoop, calls=%fused_computation.7.clone.1 | loop fusion | bytes 3146240 | tf_op jit(solution)/shard_map/while/body/jit(dynamic_update_index_in_dim)/dynamic_update_slice | solution.py:84
  (4 shorter events, 0.1 us)
Async XLA Ops:
  16.0 24.6 %all-to-all-start = ((bf16[32,1,2,6,1024]{4,2,3,1,0:T(2,128)(2,1)}), bf16[32,1,2,6,1024]{4,2,3,1,0:T(2,128)(2,1)S(1)}, u32[]{:S(2)}, u32[]{:S(2)}) async-start(bf16[32,1,2,6,1024]{4,2,3,1,0:T(2,128)(2,1)} %copy.97), calls=%async_computation | async-start | bytes 1572864 | tf_op jit(solution)/shard_map/all_to_all | solution.py:68
where the time goes:
time: 184 us; the launch traced here: 180 us
  local copies, waits for them, and re-layouts  101 us (55%)
  matrix products  38 us (21%)
  waiting for transfers between devices  17.4 us (9%)
  other arithmetic  17 us (9%)
  starting transfers between devices  6.3 us (3%)
    reshape x2, local copies, waits for them, and re-layouts, one_block(): images = images.reshape(NZ, 2 * COILS, column_total // COILS)  39.2 us
    convert_element_type x2, local copies, waits for them, and re-layouts, one_block(): jnp.dot(table, block, preferred_element_type=jnp.float32)  33.3 us
    dot_general x2, matrix products, one_block(): lax.dot_general(images, images, (((2,), (2,)), ((0,), (0,))), preferred_e...  25.3 us
    all_to_all x1, waiting for transfers between devices, local(): lax.all_to_all(local_window, 'slab', split_axis=0, concat_axis=4, tiled=T...  17.4 us
    dot_general x2, local copies, waits for them, and re-layouts, one_block(): lax.dot_general(images, images, (((2,), (2,)), ((0,), (0,))), preferred_e...  13.4 us
    dot_general x2, matrix products, one_block(): jnp.dot(table, block, preferred_element_type=jnp.float32)  12.7 us
    dynamic_update_slice x4, local copies, waits for them, and re-layouts, local(): grams = lax.map(one_block, blocks)  8.9 us
    another operation x4, other arithmetic  8.38 us
  transfers between devices with their start and end apart: 1, of which 1 were waited for; matrix products, arithmetic and copies ran while one was open for 0% of the time, Pallas kernels for 0%

commit v1 on v0

v1 whole, which is shorter than its diff:
```python
import functools
import math

import jax
import jax.numpy as jnp
import numpy as np
from jax import lax
from jax.experimental import pallas as pl
from jax.experimental.pallas import tpu as pltpu
from jax.sharding import PartitionSpec as P

COILS = 32
TAP = 6
NY = 256
NZ = 192
XD = 2
YLO = 127
SUB = 8
ROW = 2 * TAP
PADROW = 16
LANES = 128

full_turn = 2.0 * math.pi


def split(value):
    value = np.asarray(value, np.float32)
    high = value.astype(jnp.bfloat16)
    low = (value - high.astype(np.float32)).astype(jnp.bfloat16)
    return high, low


def plane_matrix(planes, halves):
    count = planes // XD
    angle = (np.arange(planes)[:, None] * np.arange(TAP)[None] % planes) * (full_turn / planes)
    cosine, sine = np.cos(angle), np.sin(angle)
    base = np.zeros((planes, 2, TAP, 2, TAP, SUB))
    for w in range(TAP):
        base[:, 0, w, 0, :, w] = cosine
        base[:, 0, w, 1, :, w] = -sine
        base[:, 1, w, 0, :, w] = sine
        base[:, 1, w, 1, :, w] = cosine
    high, low = split(base.reshape(count, XD * ROW, 2 * TAP * SUB))
    terms = np.concatenate([high, low, high], axis=2)
    depth = terms.shape[2]
    full = np.zeros((count, halves, XD * ROW, halves, depth), terms.dtype)
    for half in range(halves):
        full[:, half, :, half, :] = terms
    return full.reshape(count * halves * XD * ROW, halves * depth)


def place_matrix(halves):
    full = np.zeros((XD, halves, PADROW, halves, XD, ROW), np.float32)
    for plane in range(XD):
        for half in range(halves):
            for row in range(ROW):
                full[plane, half, row, half, plane, row] = 1
    return full.reshape(XD * halves * PADROW, halves * XD * ROW).astype(jnp.bfloat16)


def swap_matrix():
    full = np.zeros((ROW, COILS, COILS, PADROW), np.float32)
    for row in range(ROW):
        for coil in range(COILS):
            full[row, coil, coil, row] = 1
    return full.reshape(ROW * COILS, COILS * PADROW).astype(jnp.bfloat16)


def depth_matrix():
    angle = (np.arange(NZ)[:, None] * np.arange(TAP)[None] % NZ).astype(np.float32) * np.float32(full_turn / NZ)
    cosine = np.cos(angle).astype(jnp.bfloat16).astype(np.float32)
    sine = np.sin(angle).astype(jnp.bfloat16).astype(np.float32)
    alpha = np.concatenate([cosine, -sine], axis=1)
    beta = np.concatenate([sine, cosine], axis=1)
    full = np.zeros((2, NZ, ROW, PADROW), np.float32)
    full[0, :, :, :ROW] = alpha[:, :, None] * alpha[:, None, :] + beta[:, :, None] * beta[:, None, :]
    full[1, :, :, :ROW] = beta[:, :, None] * alpha[:, None, :] - alpha[:, :, None] * beta[:, None, :]
    high, low = split(full.reshape(2 * NZ, ROW * PADROW))
    return np.concatenate([high, low, high], axis=1)


def exchange_kernel(count, halves, width, kernels, planes, place, out, taps, terms, sent, held, send_sem, recv_sem):
    me = lax.axis_index("slab")
    barrier = pltpu.get_barrier_semaphore()

    def greet(step, carry):
        pl.semaphore_signal(
            barrier, inc=1, device_id={"slab": lax.rem(me + step, count)}, device_id_type=pl.DeviceIdType.MESH
        )
        return carry

    lax.fori_loop(1, count, greet, 0)

    lanes = kernels.shape[4]
    taps[...] = jnp.zeros_like(taps)
    for u in range(TAP):
        real_sum = jnp.zeros((TAP, lanes), jnp.float32)
        imag_sum = jnp.zeros((TAP, lanes), jnp.float32)
        for v in range(TAP):
            angle = (v * YLO % NY) * (full_turn / NY)
            cosine, sine = math.cos(angle), math.sin(angle)
            real_tap = kernels[0, u, v].astype(jnp.float32)
            imag_tap = kernels[1, u, v].astype(jnp.float32)
            real_sum = real_sum + real_tap * cosine - imag_tap * sine
            imag_sum = imag_sum + real_tap * sine + imag_tap * cosine
        taps[u * SUB : u * SUB + TAP, :] = real_sum
        taps[(TAP + u) * SUB : (TAP + u) * SUB + TAP, :] = imag_sum
    depth = 2 * TAP * SUB
    for half in range(halves):
        value = taps[:, half * width : (half + 1) * width]
        high = value.astype(jnp.bfloat16)
        low = (value - high.astype(jnp.float32)).astype(jnp.bfloat16)
        start = half * 3 * depth
        terms[start : start + depth, :] = high
        terms[start + depth : start + 2 * depth, :] = high
        terms[start + 2 * depth : start + 3 * depth, :] = low
    rows = halves * XD * ROW
    images = jnp.dot(planes[...], terms[...], preferred_element_type=jnp.float32)
    sent[...] = images.astype(jnp.bfloat16).reshape(count, rows, width)

    pl.semaphore_wait(barrier, count - 1)

    def copy_to(step):
        return pltpu.make_async_remote_copy(
            src_ref=sent.at[lax.rem(me + step, count)],
            dst_ref=held.at[step],
            send_sem=send_sem.at[step],
            recv_sem=recv_sem.at[step],
            device_id={"slab": lax.rem(me + step, count)},
            device_id_type=pl.DeviceIdType.MESH,
        )

    def send(step, carry):
        copy_to(step).start()
        return carry

    lax.fori_loop(1, count, send, 0)

    column_count = count * lanes // COILS

    def settle(source, block):
        moved = jnp.dot(place[...], block, preferred_element_type=jnp.float32).astype(jnp.bfloat16)
        size = halves * PADROW
        coil = source * lanes // column_count
        column = pl.multiple_of(lax.rem(source * lanes, column_count), width)
        for plane in range(XD):
            out[plane, pl.ds(pl.multiple_of(coil * PADROW, PADROW), size), pl.ds(column, width)] = moved[
                plane * size : (plane + 1) * size
            ]

    settle(me, sent[me])

    def receive(step, carry):
        copy_to(step).wait_recv()
        settle(lax.rem(me - step + count, count), held[step])
        return carry

    lax.fori_loop(1, count, receive, 0)

    def drain(step, carry):
        copy_to(step).wait_send()
        return carry

    lax.fori_loop(1, count, drain, 0)


def gram_kernel(taps, swap, table, out, spread, right):
    group = LANES // COILS
    ordered = jnp.dot(swap[...], taps[0], preferred_element_type=jnp.float32).astype(jnp.bfloat16)
    for row in range(ROW):
        block = ordered[row * COILS : (row + 1) * COILS]
        for copy in range(group):
            start = (row * group + copy) * COILS
            spread[start : start + COILS, :] = block
    lane = lax.broadcasted_iota(jnp.int32, (PADROW, LANES), 1) // COILS
    size = ROW * PADROW
    pair = 2
    for row in range(0, ROW, pair):
        products = lax.dot_general(
            taps[0],
            spread[row * LANES : (row + pair) * LANES, :],
            (((1,), (1,)), ((), ())),
            preferred_element_type=jnp.float32,
        )
        for side in range(pair):
            start = (row + side) * PADROW
            for block in range(COILS // group):
                picked = None
                for member in range(group):
                    first = (block * group + member) * PADROW
                    piece = products[first : first + PADROW, side * LANES : (side + 1) * LANES]
                    picked = piece if picked is None else jnp.where(lane == member, piece, picked)
                high = picked.astype(jnp.bfloat16)
                low = (picked - high.astype(jnp.float32)).astype(jnp.bfloat16)
                columns = slice(block * LANES, (block + 1) * LANES)
                right[start : start + PADROW, columns] = high
                right[size + start : size + start + PADROW, columns] = high
                right[2 * size + start : 2 * size + start + PADROW, columns] = low
    for part in range(2):
        out[part, 0, 0] = jnp.dot(
            table[part * NZ : (part + 1) * NZ, :], right[...], preferred_element_type=jnp.float32
        )


def local(kernels):
    count = lax.axis_size("slab")
    lanes = kernels.shape[4]
    column_count = count * lanes // COILS
    halves = max(1, lanes // column_count)
    width = lanes // halves
    rows = halves * XD * ROW
    depth = 2 * TAP * SUB
    vmem = pl.BlockSpec(memory_space=pltpu.VMEM)
    taps = pl.pallas_call(
        functools.partial(exchange_kernel, count, halves, width),
        out_shape=jax.ShapeDtypeStruct((XD, COILS * PADROW, column_count), jnp.bfloat16),
        in_specs=[vmem] * 3,
        out_specs=vmem,
        scratch_shapes=[
            pltpu.VMEM((depth, lanes), jnp.float32),
            pltpu.VMEM((halves * 3 * depth, width), jnp.bfloat16),
            pltpu.VMEM((count, rows, width), jnp.bfloat16),
            pltpu.VMEM((count, rows, width), jnp.bfloat16),
            pltpu.SemaphoreType.DMA((count,)),
            pltpu.SemaphoreType.DMA((count,)),
        ],
        compiler_params=pltpu.CompilerParams(collective_id=0, has_side_effects=True),
        name="exchange",
    )(kernels, jnp.asarray(plane_matrix(XD * count, halves)), jnp.asarray(place_matrix(halves)))
    wide = COILS * PADROW
    return pl.pallas_call(
        gram_kernel,
        grid=(XD,),
        out_shape=jax.ShapeDtypeStruct((2, XD, 1, NZ, COILS * COILS), jnp.float32),
        in_specs=[
            pl.BlockSpec((1, wide, column_count), lambda plane: (plane, 0, 0)),
            pl.BlockSpec((ROW * COILS, wide), lambda plane: (0, 0)),
            pl.BlockSpec((2 * NZ, 3 * ROW * PADROW), lambda plane: (0, 0)),
        ],
        out_specs=pl.BlockSpec((2, 1, 1, NZ, COILS * COILS), lambda plane: (0, plane, 0, 0, 0)),
        scratch_shapes=[
            pltpu.VMEM((ROW * LANES, column_count), jnp.bfloat16),
            pltpu.VMEM((3 * ROW * PADROW, COILS * COILS), jnp.bfloat16),
        ],
        name="gram",
    )(taps, jnp.asarray(swap_matrix()), jnp.asarray(depth_matrix()))


def solution(mesh):
    return jax.shard_map(
        local,
        mesh=mesh,
        in_specs=(P("scan", None, None, None, "slab"),),
        out_specs=P("scan", "slab", None, None, None),
        check_vma=False,
    )
```

time: 184 us -> 34.4 us (0.19); the launches traced: 180 us -> 34.2 us
  local copies, waits for them, and re-layouts: 101 us -> 2.46 us
  matrix products: 38 us -> 0 us
  Pallas kernels: 0 us -> 31.8 us
  waiting for transfers between devices: 17.4 us -> 0 us
  other arithmetic: 17 us -> 0 us
  starting transfers between devices: 6.3 us -> 0 us
    reshape x2 -> x0, local copies, waits for them, and re-layouts: 39.2 us -> none  [one_block(): images = images.reshape(NZ, 2 * COILS, column_total // COILS)]
    dot_general x4 -> x0, matrix products: 38 us -> none  [the longest x2 25.3 us: one_block(): lax.dot_general(images, images, (((2,), (2,)), ((0,), (0,))), preferred_e...]
    convert_element_type x3 -> x0, local copies, waits for them, and re-layouts: 33.5 us -> none  [the longest x2 33.3 us: one_block(): jnp.dot(table, block, preferred_element_type=jnp.float32)]
    pallas_call x0 -> x2, Pallas kernels: none -> 31.8 us  [the longest x1 25.3 us: local(): pl.pallas_call(functools.partial(exchange_kernel, count, halves, width),...]
    all_to_all x1 -> x0, waiting for transfers between devices: 17.4 us -> none  [local(): lax.all_to_all(local_window, 'slab', split_axis=0, concat_axis=4, tiled=T...]
    dot_general x2 -> x0, local copies, waits for them, and re-layouts: 13.4 us -> none  [one_block(): lax.dot_general(images, images, (((2,), (2,)), ((0,), (0,))), preferred_e...]
    another operation x11 -> x0, other arithmetic: 11 us -> none
    dynamic_update_slice x4 -> x0, local copies, waits for them, and re-layouts: 8.9 us -> none  [local(): grams = lax.map(one_block, blocks)]
  transfers between devices with their start and end apart: 1 -> 0, of which waited for: 1 -> 0; matrix products, arithmetic and copies ran while one was open for 0% -> 0% of each run, Pallas kernels for 0% -> 0%
where the time goes in v1:
time: 34.4 us; the launch traced here: 34.2 us
  Pallas kernels  31.8 us (92%)
  local copies, waits for them, and re-layouts  2.46 us (7%)
    pallas_call x1, Pallas kernels, local(): pl.pallas_call(functools.partial(exchange_kernel, count, halves, width),...  25.3 us
    pallas_call x1, Pallas kernels, local(): pl.pallas_call(gram_kernel, grid=(XD,), out_shape=jax.ShapeDtypeStruct((2...  6.49 us
    unnamed x1, local copies, waits for them, and re-layouts  2.46 us

profile of v1, /device:TPU:29, one launch (start us, length us, event | category | flops | bytes accessed | tf_op | source)
XLA Modules:
  0.0 34.2 jit_solution(578127647551172440)
XLA Ops:
  0.0 2.5 %copy.6.kernels = bf16[2,6,6,6,1024]{4,3,2,1,0:T(8,128)(2,1)} copy(bf16[2,6,6,6,1024]{4,0,3,2,1:T(2,128)(2,1)} %param.5) | data formatting | bytes 1769472 | tf_op args[0]
  2.5 25.3 %exchange.1.taps = bf16[2,512,512]{2,1,0:T(8,128)(2,1)} custom-call(bf16[2,6,6,6,1024]{4,3,2,1,0:T(8,128)(2,1)} %copy.6.kernels, bf16[768,576]{1,0:T(8,128)(2,1)} %constant.8.clone.planes, bf16[64,48]{1,0:T(8,128)(2,1)} %constant.9.clone.place), custom_call_target="tpu_custom_call" | custom-call | tf_op jit(solution)/shard_map/exchange/pallas_call | solution.py:214
  27.7 6.5 %gram.1 = f32[2,2,1,192,1024]{4,3,2,1,0:T(8,128)} custom-call(bf16[2,512,512]{2,1,0:T(8,128)(2,1)} %exchange.1.taps, bf16[384,512]{1,0:T(8,128)(2,1)} %constant.10.clone.swap, bf16[384,576]{1,0:T(8,128)(2,1)} %constant.11.clone.table), custom_call_target="tpu_custom_call" | custom-call | tf_op jit(solution)/shard_map/gram/pallas_call | solution.py:231

commit v2 on v1

v2 whole, which is shorter than its diff:
```python
import functools
import math

import jax
import jax.numpy as jnp
import numpy as np
from jax import lax
from jax.experimental import pallas as pl
from jax.experimental.pallas import tpu as pltpu
from jax.sharding import PartitionSpec as P

COILS = 32
TAP = 6
NY = 256
NZ = 192
XD = 2
YLO = 127
SUB = 8
ROW = 2 * TAP
PADROW = 16
LANES = 128

full_turn = 2.0 * math.pi


def split(value):
    value = np.asarray(value, np.float32)
    high = value.astype(jnp.bfloat16)
    low = (value - high.astype(np.float32)).astype(jnp.bfloat16)
    return high, low


def plane_matrix(planes):
    count = planes // XD
    grid = np.arange(planes)
    taps = np.arange(TAP)
    first = (grid[:, None] * taps[None] % planes) * (full_turn / planes)
    second = (taps * YLO % NY) * (full_turn / NY)
    angle = first[:, :, None] + second[None, None, :]
    cosine, sine = np.cos(angle), np.sin(angle)
    base = np.zeros((planes, 2, TAP, TAP, TAP, TAP, 2))
    for w in range(TAP):
        base[:, 0, w, :, :, w, 0] = cosine
        base[:, 0, w, :, :, w, 1] = -sine
        base[:, 1, w, :, :, w, 0] = sine
        base[:, 1, w, :, :, w, 1] = cosine
    base = base.reshape(count, XD, ROW, 2 * TAP**3)
    tiles = [base[:, 0, :SUB], base[:, 0, SUB:], base[:, 1, SUB:], base[:, 1, :SUB]]
    high, low = split(np.concatenate(tiles, axis=1).reshape(count * XD * ROW, 2 * TAP**3))
    return np.concatenate([high, low], axis=1)


def message_rows(plane, parts):
    if parts == 1:
        return [(0, row) for row in range(SUB)] + [
            (0, SUB + row % 4) if (row >= 4) == (plane == 1) else None for row in range(SUB)
        ]
    whole = [(part, row) for part in range(parts) for row in range(SUB)]
    return whole + [(part, row) for part in range(parts) for row in range(SUB, ROW)]


def place_matrix(parts):
    size = len(message_rows(0, parts))
    full = np.zeros((XD, parts * PADROW, size), np.float32)
    for plane in range(XD):
        for index, entry in enumerate(message_rows(plane, parts)):
            if entry is not None:
                full[plane, entry[0] * PADROW + entry[1], index] = 1
    return full.astype(jnp.bfloat16)


def pack(block, parts, width):
    first, mixed, second = block[:SUB], block[SUB : 2 * SUB], block[2 * SUB :]
    if parts == 1:
        return [jnp.concatenate([first, mixed]), jnp.concatenate([second, mixed])]
    cut = lambda value, part: value[:, part * width : (part + 1) * width]
    lower = lax.broadcasted_iota(jnp.int32, (SUB, width), 0) < SUB // 2
    turned = pltpu.roll(mixed, SUB // 2, axis=0)
    packed = []
    for plane, whole in enumerate((first, second)):
        rows = [cut(whole, part) for part in range(parts)]
        under, over = (mixed, turned) if plane == 0 else (turned, mixed)
        for part in range(0, parts, 2):
            rows.append(jnp.where(lower, cut(under, part), cut(over, part + 1)))
        packed.append(jnp.concatenate(rows))
    return packed


def swap_matrix():
    full = np.zeros((ROW, COILS, COILS, PADROW), np.float32)
    for row in range(ROW):
        for coil in range(COILS):
            full[row, coil, coil, row] = 1
    return full.reshape(ROW * COILS, COILS * PADROW).astype(jnp.bfloat16)


def depth_matrix():
    angle = (np.arange(NZ)[:, None] * np.arange(TAP)[None] % NZ).astype(np.float32) * np.float32(full_turn / NZ)
    cosine = np.cos(angle).astype(jnp.bfloat16).astype(np.float32)
    sine = np.sin(angle).astype(jnp.bfloat16).astype(np.float32)
    alpha = np.concatenate([cosine, -sine], axis=1)
    beta = np.concatenate([sine, cosine], axis=1)
    full = np.zeros((2, NZ, ROW, PADROW), np.float32)
    full[0, :, :, :ROW] = alpha[:, :, None] * alpha[:, None, :] + beta[:, :, None] * beta[:, None, :]
    full[1, :, :, :ROW] = beta[:, :, None] * alpha[:, None, :] - alpha[:, :, None] * beta[:, None, :]
    high, low = split(full.reshape(2 * NZ, ROW * PADROW))
    return np.stack([high, low]).reshape(2, 2, NZ, ROW * PADROW)


def exchange_kernel(
    count, parts, width, kernels, planes, place, swap, right, sent, held, taps, spread, send_sem, recv_sem
):
    me = lax.axis_index("slab")
    barrier = pltpu.get_barrier_semaphore()

    def greet(step, carry):
        pl.semaphore_signal(
            barrier, inc=1, device_id={"slab": lax.rem(me + step, count)}, device_id_type=pl.DeviceIdType.MESH
        )
        return carry

    lax.fori_loop(1, count, greet, 0)

    lanes = kernels.shape[2]
    depth = 2 * TAP**3
    rows = XD * ROW
    columns = kernels[...].reshape(depth, lanes)
    images = jnp.dot(planes[:, :depth], columns, preferred_element_type=jnp.float32)
    images = images + jnp.dot(planes[:, depth:], columns, preferred_element_type=jnp.float32)
    for target in range(count):
        for plane, message in enumerate(pack(images[target * rows : (target + 1) * rows], parts, width)):
            sent[plane, target] = message.astype(jnp.bfloat16)

    pl.semaphore_wait(barrier, count - 1)

    def copy_to(plane, step):
        target = lax.rem(me + step, count)
        return pltpu.make_async_remote_copy(
            src_ref=sent.at[plane, target],
            dst_ref=held.at[plane, step],
            send_sem=send_sem.at[plane, step],
            recv_sem=recv_sem.at[plane, step],
            device_id={"slab": target},
            device_id_type=pl.DeviceIdType.MESH,
        )

    for plane in range(XD):

        def send(step, carry):
            copy_to(plane, step).start()
            return carry

        lax.fori_loop(1, count, send, 0)

    column_count = count * lanes // COILS

    def settle(plane, source, block):
        moved = jnp.dot(place[plane], block, preferred_element_type=jnp.float32).astype(jnp.bfloat16)
        for part in range(parts):
            start = source * lanes + part * width
            coil = start // column_count
            column = pl.multiple_of(lax.rem(start, column_count), width)
            taps[pl.ds(pl.multiple_of(coil * PADROW, PADROW), PADROW), pl.ds(column, width)] = moved[
                part * PADROW : (part + 1) * PADROW
            ]

    for plane in range(XD):
        settle(plane, me, sent[plane, me])

        def receive(step, carry):
            copy_to(plane, step).wait_recv()
            settle(plane, lax.rem(me - step + count, count), held[plane, step])
            return carry

        lax.fori_loop(1, count, receive, 0)
        gram_products(taps, swap, right.at[plane], spread)

    for plane in range(XD):

        def drain(step, carry):
            copy_to(plane, step).wait_send()
            return carry

        lax.fori_loop(1, count, drain, 0)


def gram_products(taps, swap, right, spread):
    group = LANES // COILS
    ordered = jnp.dot(swap[...], taps[...], preferred_element_type=jnp.float32).astype(jnp.bfloat16)
    for row in range(ROW):
        block = ordered[row * COILS : (row + 1) * COILS]
        for copy in range(group):
            start = (row * group + copy) * COILS
            spread[start : start + COILS, :] = block
    lane = lax.broadcasted_iota(jnp.int32, (PADROW, LANES), 1) // COILS
    pair = 2
    for row in range(0, ROW, pair):
        products = lax.dot_general(
            taps[...],
            spread[row * LANES : (row + pair) * LANES, :],
            (((1,), (1,)), ((), ())),
            preferred_element_type=jnp.float32,
        )
        for side in range(pair):
            start = (row + side) * PADROW
            for block in range(COILS // group):
                picked = None
                for member in range(group):
                    first = (block * group + member) * PADROW
                    piece = products[first : first + PADROW, side * LANES : (side + 1) * LANES]
                    picked = piece if picked is None else jnp.where(lane == member, piece, picked)
                high = picked.astype(jnp.bfloat16)
                low = (picked - high.astype(jnp.float32)).astype(jnp.bfloat16)
                columns = slice(block * LANES, (block + 1) * LANES)
                right[0, start : start + PADROW, columns] = high
                right[1, start : start + PADROW, columns] = low


def depth_kernel(right, table, out):
    left = jnp.concatenate([table[0, 0], table[1, 0], table[0, 0]], axis=1)
    stack = jnp.concatenate([right[0, 0], right[0, 0], right[0, 1]], axis=0)
    out[0, 0, 0] = jnp.dot(left, stack, preferred_element_type=jnp.float32)


def local(kernels):
    count = lax.axis_size("slab")
    lanes = kernels.shape[4]
    column_count = count * lanes // COILS
    parts = 4 if lanes % (4 * LANES) == 0 else 1
    width = lanes // parts
    size = len(message_rows(0, parts))
    depth = ROW * PADROW
    vmem = pl.BlockSpec(memory_space=pltpu.VMEM)
    columns = jnp.transpose(kernels, (1, 2, 3, 0, 4)).reshape(TAP**3, 2, lanes)
    right = pl.pallas_call(
        functools.partial(exchange_kernel, count, parts, width),
        out_shape=jax.ShapeDtypeStruct((XD, 2, depth, COILS * COILS), jnp.bfloat16),
        in_specs=[vmem] * 4,
        out_specs=vmem,
        scratch_shapes=[
            pltpu.VMEM((XD, count, size, width), jnp.bfloat16),
            pltpu.VMEM((XD, count, size, width), jnp.bfloat16),
            pltpu.VMEM((COILS * PADROW, column_count), jnp.bfloat16),
            pltpu.VMEM((ROW * LANES, column_count), jnp.bfloat16),
            pltpu.SemaphoreType.DMA((XD, count)),
            pltpu.SemaphoreType.DMA((XD, count)),
        ],
        compiler_params=pltpu.CompilerParams(collective_id=0, has_side_effects=True),
        name="exchange",
    )(columns, jnp.asarray(plane_matrix(XD * count)), jnp.asarray(place_matrix(parts)), jnp.asarray(swap_matrix()))
    return pl.pallas_call(
        depth_kernel,
        grid=(XD, 2),
        out_shape=jax.ShapeDtypeStruct((2, XD, 1, NZ, COILS * COILS), jnp.float32),
        in_specs=[
            pl.BlockSpec((1, 2, depth, COILS * COILS), lambda plane, part: (plane, 0, 0, 0)),
            pl.BlockSpec((2, 1, NZ, depth), lambda plane, part: (0, part, 0, 0)),
        ],
        out_specs=pl.BlockSpec((1, 1, 1, NZ, COILS * COILS), lambda plane, part: (part, plane, 0, 0, 0)),
        name="depth",
    )(right, jnp.asarray(depth_matrix()))


def solution(mesh):
    return jax.shard_map(
        local,
        mesh=mesh,
        in_specs=(P("scan", None, None, None, "slab"),),
        out_specs=P("scan", "slab", None, None, None),
        check_vma=False,
    )
```

time: 34.4 us -> 32.4 us (0.942)
  local copies, waits for them, and re-layouts: 2.46 us -> 0 us
  Pallas kernels: 31.8 us -> 32.2 us
    unnamed x1 -> x0, local copies, waits for them, and re-layouts: 2.46 us -> none
    pallas_call x2, Pallas kernels: 31.8 us -> 32.2 us  [the longest x1 27 us: local(): pl.pallas_call(functools.partial(exchange_kernel, count, parts, width), o...]
where the time goes in v2:
time: 32.4 us; the launch traced here: 32.2 us
  Pallas kernels  32.2 us (99%)
    pallas_call x1, Pallas kernels, local(): pl.pallas_call(functools.partial(exchange_kernel, count, parts, width), o...  27 us
    pallas_call x1, Pallas kernels, local(): pl.pallas_call(depth_kernel, grid=(XD, 2), out_shape=jax.ShapeDtypeStruct...  5.18 us

profile of v2, /device:TPU:29, one launch (start us, length us, event | category | flops | bytes accessed | tf_op | source)
XLA Modules:
  0.0 32.2 jit_solution(56079240474192573)
XLA Ops:
  0.0 27.0 %exchange.1.right = bf16[2,2,192,1024]{3,2,1,0:T(8,128)(2,1)} custom-call(bf16[216,2,1024]{2,1,0:T(2,128)(2,1)} %bitcast.3, bf16[384,864]{1,0:T(8,128)(2,1)} %constant.8.clone.planes, bf16[2,64,48]{2,1,0:T(8,128)(2,1)} %constant.9.clone.place, bf16[384,512]{1,0:T(8,128)(2,1)} %constant.10.clone.swap), custom_call_target="tpu_custom_call" | custom-call | tf_op jit(solution)/shard_map/exchange/pallas_call | solution.py:235
  27.0 5.2 %depth.1 = f32[2,2,1,192,1024]{4,3,2,1,0:T(8,128)} custom-call(bf16[2,2,192,1024]{3,2,1,0:T(8,128)(2,1)} %exchange.1.right, bf16[2,2,192,192]{3,2,1,0:T(8,128)(2,1)} %constant.11.clone.table), custom_call_target="tpu_custom_call" | custom-call | tf_op jit(solution)/shard_map/depth/pallas_call | solution.py:251

commit v3 on v2

--- a/solution.py
+++ b/solution.py
@@ -50,6 +50,10 @@
     return np.concatenate([high, low], axis=1)
 
 
+def slot(row):
+    return row // TAP * SUB + TAP - 1 - row % TAP
+
+
 def message_rows(plane, parts):
     if parts == 1:
         return [(0, row) for row in range(SUB)] + [
@@ -65,7 +69,7 @@
     for plane in range(XD):
         for index, entry in enumerate(message_rows(plane, parts)):
             if entry is not None:
-                full[plane, entry[0] * PADROW + entry[1], index] = 1
+                full[plane, entry[0] * PADROW + slot(entry[1]), index] = 1
     return full.astype(jnp.bfloat16)
 
 
@@ -90,25 +94,24 @@
     full = np.zeros((ROW, COILS, COILS, PADROW), np.float32)
     for row in range(ROW):
         for coil in range(COILS):
-            full[row, coil, coil, row] = 1
+            full[row, coil, coil, slot(row)] = 1
     return full.reshape(ROW * COILS, COILS * PADROW).astype(jnp.bfloat16)
 
 
 def depth_matrix():
-    angle = (np.arange(NZ)[:, None] * np.arange(TAP)[None] % NZ).astype(np.float32) * np.float32(full_turn / NZ)
-    cosine = np.cos(angle).astype(jnp.bfloat16).astype(np.float32)
-    sine = np.sin(angle).astype(jnp.bfloat16).astype(np.float32)
-    alpha = np.concatenate([cosine, -sine], axis=1)
-    beta = np.concatenate([sine, cosine], axis=1)
-    full = np.zeros((2, NZ, ROW, PADROW), np.float32)
-    full[0, :, :, :ROW] = alpha[:, :, None] * alpha[:, None, :] + beta[:, :, None] * beta[:, None, :]
-    full[1, :, :, :ROW] = beta[:, :, None] * alpha[:, None, :] - alpha[:, :, None] * beta[:, None, :]
-    high, low = split(full.reshape(2 * NZ, ROW * PADROW))
-    return np.stack([high, low]).reshape(2, 2, NZ, ROW * PADROW)
+    shift = np.arange(2 * TAP - 1) - (TAP - 1)
+    angle = (np.arange(NZ)[:, None] * shift[None] % NZ) * (full_turn / NZ)
+    full = np.zeros((2, NZ, 2, PADROW))
+    full[0, :, 0, : 2 * TAP - 1] = np.cos(angle)
+    full[0, :, 1, : 2 * TAP - 1] = -np.sin(angle)
+    full[1, :, 0, : 2 * TAP - 1] = np.sin(angle)
+    full[1, :, 1, : 2 * TAP - 1] = np.cos(angle)
+    high, low = split(full.reshape(2 * NZ, 2 * PADROW))
+    return np.concatenate([high, low, high], axis=1)
 
 
 def exchange_kernel(
-    count, parts, width, kernels, planes, place, swap, right, sent, held, taps, spread, send_sem, recv_sem
+    count, parts, width, kernels, planes, place, swap, right, sent, held, taps, send_sem, recv_sem
 ):
     me = lax.axis_index("slab")
     barrier = pltpu.get_barrier_semaphore()
@@ -173,7 +176,7 @@
             return carry
 
         lax.fori_loop(1, count, receive, 0)
-        gram_products(taps, swap, right.at[plane], spread)
+        gram_products(taps, swap, right.at[plane])
 
     for plane in range(XD):
 
@@ -184,42 +187,52 @@
         lax.fori_loop(1, count, drain, 0)
 
 
-def gram_products(taps, swap, right, spread):
+def gram_products(taps, swap, right):
     group = LANES // COILS
     ordered = jnp.dot(swap[...], taps[...], preferred_element_type=jnp.float32).astype(jnp.bfloat16)
-    for row in range(ROW):
-        block = ordered[row * COILS : (row + 1) * COILS]
-        for copy in range(group):
-            start = (row * group + copy) * COILS
-            spread[start : start + COILS, :] = block
-    lane = lax.broadcasted_iota(jnp.int32, (PADROW, LANES), 1) // COILS
-    pair = 2
-    for row in range(0, ROW, pair):
-        products = lax.dot_general(
-            taps[...],
-            spread[row * LANES : (row + pair) * LANES, :],
-            (((1,), (1,)), ((), ())),
-            preferred_element_type=jnp.float32,
-        )
-        for side in range(pair):
-            start = (row + side) * PADROW
-            for block in range(COILS // group):
-                picked = None
+    products = lax.dot_general(
+        taps[...], ordered, (((1,), (1,)), ((), ())), preferred_element_type=jnp.float32
+    )
+    lane = lax.broadcasted_iota(jnp.int32, (SUB, LANES), 1) // COILS
+    level = lax.broadcasted_iota(jnp.int32, (SUB, LANES), 0)
+    for block in range(COILS // group):
+        picked = [[None] * ROW for _ in range(2)]
+        for part in range(2):
+            for row in range(ROW):
+                place, start = row % group, row // group * LANES
                 for member in range(group):
-                    first = (block * group + member) * PADROW
-                    piece = products[first : first + PADROW, side * LANES : (side + 1) * LANES]
-                    picked = piece if picked is None else jnp.where(lane == member, piece, picked)
-                high = picked.astype(jnp.bfloat16)
-                low = (picked - high.astype(jnp.float32)).astype(jnp.bfloat16)
-                columns = slice(block * LANES, (block + 1) * LANES)
-                right[0, start : start + PADROW, columns] = high
-                right[1, start : start + PADROW, columns] = low
+                    first = (block * group + member) * PADROW + part * SUB
+                    piece = products[first : first + SUB, start : start + LANES]
+                    turn = (member - place) % group * COILS
+                    piece = pltpu.roll(piece, turn, axis=1) if turn else piece
+                    known = picked[part][row]
+                    picked[part][row] = piece if known is None else jnp.where(lane == member, piece, known)
+        columns = slice(block * LANES, (block + 1) * LANES)
+        for part in range(2):
+            under, over = None, jnp.zeros((SUB, LANES), jnp.float32)
+            for w in range(TAP):
+                if part == 0:
+                    value = picked[0][w] + picked[1][TAP + w]
+                else:
+                    value = picked[0][TAP + w] - picked[1][w]
+                if w == 0:
+                    under = value
+                    continue
+                value = pltpu.roll(value, w, axis=0)
+                under = under + jnp.where(level >= w, value, 0.0)
+                over = over + jnp.where(level < w, value, 0.0)
+            right[part * PADROW : part * PADROW + SUB, columns] = under
+            right[part * PADROW + SUB : (part + 1) * PADROW, columns] = over
 
 
 def depth_kernel(right, table, out):
-    left = jnp.concatenate([table[0, 0], table[1, 0], table[0, 0]], axis=1)
-    stack = jnp.concatenate([right[0, 0], right[0, 0], right[0, 1]], axis=0)
-    out[0, 0, 0] = jnp.dot(left, stack, preferred_element_type=jnp.float32)
+    value = right[0]
+    high = value.astype(jnp.bfloat16)
+    low = (value - high.astype(jnp.float32)).astype(jnp.bfloat16)
+    stack = jnp.concatenate([high, high, low], axis=0)
+    result = jnp.dot(table[...], stack, preferred_element_type=jnp.float32)
+    out[0, 0, 0] = result[:NZ]
+    out[1, 0, 0] = result[NZ:]
 
 
 def local(kernels):
@@ -229,19 +242,18 @@
     parts = 4 if lanes % (4 * LANES) == 0 else 1
     width = lanes // parts
     size = len(message_rows(0, parts))
-    depth = ROW * PADROW
+    pairs = COILS * COILS
     vmem = pl.BlockSpec(memory_space=pltpu.VMEM)
     columns = jnp.transpose(kernels, (1, 2, 3, 0, 4)).reshape(TAP**3, 2, lanes)
     right = pl.pallas_call(
         functools.partial(exchange_kernel, count, parts, width),
-        out_shape=jax.ShapeDtypeStruct((XD, 2, depth, COILS * COILS), jnp.bfloat16),
+        out_shape=jax.ShapeDtypeStruct((XD, 2 * PADROW, pairs), jnp.float32),
         in_specs=[vmem] * 4,
         out_specs=vmem,
         scratch_shapes=[
             pltpu.VMEM((XD, count, size, width), jnp.bfloat16),
             pltpu.VMEM((XD, count, size, width), jnp.bfloat16),
             pltpu.VMEM((COILS * PADROW, column_count), jnp.bfloat16),
-            pltpu.VMEM((ROW * LANES, column_count), jnp.bfloat16),
             pltpu.SemaphoreType.DMA((XD, count)),
             pltpu.SemaphoreType.DMA((XD, count)),
         ],
@@ -251,12 +263,12 @@
     return pl.pallas_call(
         depth_kernel,
         grid=(XD, 2),
-        out_shape=jax.ShapeDtypeStruct((2, XD, 1, NZ, COILS * COILS), jnp.float32),
+        out_shape=jax.ShapeDtypeStruct((2, XD, 1, NZ, pairs), jnp.float32),
         in_specs=[
-            pl.BlockSpec((1, 2, depth, COILS * COILS), lambda plane, part: (plane, 0, 0, 0)),
-            pl.BlockSpec((2, 1, NZ, depth), lambda plane, part: (0, part, 0, 0)),
+            pl.BlockSpec((1, 2 * PADROW, pairs // 2), lambda plane, side: (plane, 0, side)),
+            pl.BlockSpec((2 * NZ, 6 * PADROW), lambda plane, side: (0, 0)),
         ],
-        out_specs=pl.BlockSpec((1, 1, 1, NZ, COILS * COILS), lambda plane, part: (part, plane, 0, 0, 0)),
+        out_specs=pl.BlockSpec((2, 1, 1, NZ, pairs // 2), lambda plane, side: (0, plane, 0, 0, side)),
         name="depth",
     )(right, jnp.asarray(depth_matrix()))
 

time: 32.4 us -> 30.9 us (0.954)
  Pallas kernels: 32.2 us -> 30.6 us
    pallas_call x1, Pallas kernels: 5.18 us -> 4.04 us  [local(): pl.pallas_call(depth_kernel, grid=(XD, 2), out_shape=jax.ShapeDtypeStruct...]
    pallas_call x1, Pallas kernels: 27 us -> 26.5 us  [local(): pl.pallas_call(functools.partial(exchange_kernel, count, parts, width), o...]
where the time goes in v3:
time: 30.9 us; the launch traced here: 30.6 us
  Pallas kernels  30.6 us (99%)
    pallas_call x1, Pallas kernels, local(): pl.pallas_call(functools.partial(exchange_kernel, count, parts, width), o...  26.5 us
    pallas_call x1, Pallas kernels, local(): pl.pallas_call(depth_kernel, grid=(XD, 2), out_shape=jax.ShapeDtypeStruct...  4.04 us

profile of v3, /device:TPU:29, one launch (start us, length us, event | category | flops | bytes accessed | tf_op | source)
XLA Modules:
  0.0 30.6 jit_solution(2313480687114131116)
XLA Ops:
  0.0 26.5 %exchange.1.right = f32[2,32,1024]{2,1,0:T(8,128)} custom-call(bf16[216,2,1024]{2,1,0:T(2,128)(2,1)} %bitcast.3, bf16[384,864]{1,0:T(8,128)(2,1)} %constant.8.clone.planes, bf16[2,64,48]{2,1,0:T(8,128)(2,1)} %constant.9.clone.place, bf16[384,512]{1,0:T(8,128)(2,1)} %constant.10.clone.swap), custom_call_target="tpu_custom_call" | custom-call | tf_op jit(solution)/shard_map/exchange/pallas_call | solution.py:248
  26.5 4.0 %depth.1 = f32[2,2,1,192,1024]{4,3,2,1,0:T(8,128)} custom-call(f32[2,32,1024]{2,1,0:T(8,128)} %exchange.1.right, bf16[384,96]{1,0:T(8,128)(2,1)} %constant.11.clone.table), custom_call_target="tpu_custom_call" | custom-call | tf_op jit(solution)/shard_map/depth/pallas_call | solution.py:263

commit v4 on v3

--- a/solution.py
+++ b/solution.py
@@ -107,7 +107,7 @@
     full[1, :, 0, : 2 * TAP - 1] = np.sin(angle)
     full[1, :, 1, : 2 * TAP - 1] = np.cos(angle)
     high, low = split(full.reshape(2 * NZ, 2 * PADROW))
-    return np.concatenate([high, low, high], axis=1)
+    return np.concatenate([high, low, high], axis=1).reshape(2, NZ, 6 * PADROW)
 
 
 def exchange_kernel(
@@ -123,6 +123,11 @@
         return carry
 
     lax.fori_loop(1, count, greet, 0)
+
+    def partner(step, sign):
+        if count & (count - 1) == 0:
+            return me ^ step
+        return lax.rem(me + sign * step + count, count)
 
     lanes = kernels.shape[2]
     depth = 2 * TAP**3
@@ -137,7 +142,7 @@
     pl.semaphore_wait(barrier, count - 1)
 
     def copy_to(plane, step):
-        target = lax.rem(me + step, count)
+        target = partner(step, 1)
         return pltpu.make_async_remote_copy(
             src_ref=sent.at[plane, target],
             dst_ref=held.at[plane, step],
@@ -172,7 +177,7 @@
 
         def receive(step, carry):
             copy_to(plane, step).wait_recv()
-            settle(plane, lax.rem(me - step + count, count), held[plane, step])
+            settle(plane, partner(step, -1), held[plane, step])
             return carry
 
         lax.fori_loop(1, count, receive, 0)
@@ -230,9 +235,8 @@
     high = value.astype(jnp.bfloat16)
     low = (value - high.astype(jnp.float32)).astype(jnp.bfloat16)
     stack = jnp.concatenate([high, high, low], axis=0)
-    result = jnp.dot(table[...], stack, preferred_element_type=jnp.float32)
-    out[0, 0, 0] = result[:NZ]
-    out[1, 0, 0] = result[NZ:]
+    for part in range(2):
+        out[part, 0, 0] = jnp.dot(table[part], stack, preferred_element_type=jnp.float32)
 
 
 def local(kernels):
@@ -265,10 +269,10 @@
         grid=(XD, 2),
         out_shape=jax.ShapeDtypeStruct((2, XD, 1, NZ, pairs), jnp.float32),
         in_specs=[
-            pl.BlockSpec((1, 2 * PADROW, pairs // 2), lambda plane, side: (plane, 0, side)),
-            pl.BlockSpec((2 * NZ, 6 * PADROW), lambda plane, side: (0, 0)),
+            pl.BlockSpec((1, 2 * PADROW, pairs), lambda plane, side: (plane, 0, 0)),
+            pl.BlockSpec((2, NZ // 2, 6 * PADROW), lambda plane, side: (0, side, 0)),
         ],
-        out_specs=pl.BlockSpec((2, 1, 1, NZ, pairs // 2), lambda plane, side: (0, plane, 0, 0, side)),
+        out_specs=pl.BlockSpec((2, 1, 1, NZ // 2, pairs), lambda plane, side: (0, plane, 0, side, 0)),
         name="depth",
     )(right, jnp.asarray(depth_matrix()))
 

time: 30.9 us -> 31.7 us (1.026)
  the two profiles are of different devices: /device:TPU:29 before, /device:TPU:0 now
where the time goes in v4:
time: 31.7 us; the launch traced here: 31.4 us
  Pallas kernels  31.4 us (99%)
    pallas_call x1, Pallas kernels, local(): pl.pallas_call(functools.partial(exchange_kernel, count, parts, width), o...  27.4 us
    pallas_call x1, Pallas kernels, local(): pl.pallas_call(depth_kernel, grid=(XD, 2), out_shape=jax.ShapeDtypeStruct...  4.02 us

profile of v4, /device:TPU:0, one launch (start us, length us, event | category | flops | bytes accessed | tf_op | source)
XLA Modules:
  0.0 31.4 jit_solution(15073785434795722552)
XLA Ops:
  0.0 27.4 %exchange.1.right = f32[2,32,1024]{2,1,0:T(8,128)} custom-call(bf16[216,2,1024]{2,1,0:T(2,128)(2,1)} %bitcast.3, bf16[384,864]{1,0:T(8,128)(2,1)} %constant.8.clone.planes, bf16[2,64,48]{2,1,0:T(8,128)(2,1)} %constant.9.clone.place, bf16[384,512]{1,0:T(8,128)(2,1)} %constant.10.clone.swap), custom_call_target="tpu_custom_call" | custom-call | tf_op jit(solution)/shard_map/exchange/pallas_call | solution.py:252
  27.4 4.0 %depth.1 = f32[2,2,1,192,1024]{4,3,2,1,0:T(8,128)} custom-call(f32[2,32,1024]{2,1,0:T(8,128)} %exchange.1.right, bf16[2,192,96]{2,1,0:T(8,128)(2,1)} %constant.11.clone.table), custom_call_target="tpu_custom_call" | custom-call | tf_op jit(solution)/shard_map/depth/pallas_call | solution.py:267

commit v5 on v3

--- a/solution.py
+++ b/solution.py
@@ -45,49 +45,41 @@
         base[:, 1, w, :, :, w, 0] = sine
         base[:, 1, w, :, :, w, 1] = cosine
     base = base.reshape(count, XD, ROW, 2 * TAP**3)
-    tiles = [base[:, 0, :SUB], base[:, 0, SUB:], base[:, 1, SUB:], base[:, 1, :SUB]]
-    high, low = split(np.concatenate(tiles, axis=1).reshape(count * XD * ROW, 2 * TAP**3))
-    return np.concatenate([high, low], axis=1)
+    base = np.concatenate([base, base[:, :, SUB:]], axis=2).swapaxes(0, 1)
+    high, low = split(base.reshape(XD, count * PADROW, 2 * TAP**3))
+    return np.concatenate([high, low], axis=2)
 
 
 def slot(row):
     return row // TAP * SUB + TAP - 1 - row % TAP
 
 
-def message_rows(plane, parts):
+def message_rows(parts):
     if parts == 1:
-        return [(0, row) for row in range(SUB)] + [
-            (0, SUB + row % 4) if (row >= 4) == (plane == 1) else None for row in range(SUB)
-        ]
+        return [(0, row) for row in range(ROW)] + [None] * (PADROW - ROW)
     whole = [(part, row) for part in range(parts) for row in range(SUB)]
     return whole + [(part, row) for part in range(parts) for row in range(SUB, ROW)]
 
 
 def place_matrix(parts):
-    size = len(message_rows(0, parts))
-    full = np.zeros((XD, parts * PADROW, size), np.float32)
-    for plane in range(XD):
-        for index, entry in enumerate(message_rows(plane, parts)):
-            if entry is not None:
-                full[plane, entry[0] * PADROW + slot(entry[1]), index] = 1
+    rows = message_rows(parts)
+    full = np.zeros((parts * PADROW, len(rows)), np.float32)
+    for index, entry in enumerate(rows):
+        if entry is not None:
+            full[entry[0] * PADROW + slot(entry[1]), index] = 1
     return full.astype(jnp.bfloat16)
 
 
 def pack(block, parts, width):
-    first, mixed, second = block[:SUB], block[SUB : 2 * SUB], block[2 * SUB :]
     if parts == 1:
-        return [jnp.concatenate([first, mixed]), jnp.concatenate([second, mixed])]
+        return block
     cut = lambda value, part: value[:, part * width : (part + 1) * width]
+    whole, mixed = block[:SUB], block[SUB:]
     lower = lax.broadcasted_iota(jnp.int32, (SUB, width), 0) < SUB // 2
-    turned = pltpu.roll(mixed, SUB // 2, axis=0)
-    packed = []
-    for plane, whole in enumerate((first, second)):
-        rows = [cut(whole, part) for part in range(parts)]
-        under, over = (mixed, turned) if plane == 0 else (turned, mixed)
-        for part in range(0, parts, 2):
-            rows.append(jnp.where(lower, cut(under, part), cut(over, part + 1)))
-        packed.append(jnp.concatenate(rows))
-    return packed
+    rows = [cut(whole, part) for part in range(parts)]
+    for part in range(0, parts, 2):
+        rows.append(jnp.where(lower, cut(mixed, part), cut(mixed, part + 1)))
+    return jnp.concatenate(rows)
 
 
 def swap_matrix():
@@ -126,16 +118,6 @@
 
     lanes = kernels.shape[2]
     depth = 2 * TAP**3
-    rows = XD * ROW
-    columns = kernels[...].reshape(depth, lanes)
-    images = jnp.dot(planes[:, :depth], columns, preferred_element_type=jnp.float32)
-    images = images + jnp.dot(planes[:, depth:], columns, preferred_element_type=jnp.float32)
-    for target in range(count):
-        for plane, message in enumerate(pack(images[target * rows : (target + 1) * rows], parts, width)):
-            sent[plane, target] = message.astype(jnp.bfloat16)
-
-    pl.semaphore_wait(barrier, count - 1)
-
     def copy_to(plane, step):
         target = lax.rem(me + step, count)
         return pltpu.make_async_remote_copy(
@@ -147,7 +129,15 @@
             device_id_type=pl.DeviceIdType.MESH,
         )
 
+    columns = kernels[...].reshape(depth, lanes)
     for plane in range(XD):
+        images = jnp.dot(planes[plane, :, :depth], columns, preferred_element_type=jnp.float32)
+        images = images + jnp.dot(planes[plane, :, depth:], columns, preferred_element_type=jnp.float32)
+        for target in range(count):
+            message = pack(images[target * PADROW : (target + 1) * PADROW], parts, width)
+            sent[plane, target] = message.astype(jnp.bfloat16)
+        if plane == 0:
+            pl.semaphore_wait(barrier, count - 1)
 
         def send(step, carry):
             copy_to(plane, step).start()
@@ -158,7 +148,7 @@
     column_count = count * lanes // COILS
 
     def settle(plane, source, block):
-        moved = jnp.dot(place[plane], block, preferred_element_type=jnp.float32).astype(jnp.bfloat16)
+        moved = jnp.dot(place[...], block, preferred_element_type=jnp.float32).astype(jnp.bfloat16)
         for part in range(parts):
             start = source * lanes + part * width
             coil = start // column_count
@@ -241,7 +231,7 @@
     column_count = count * lanes // COILS
     parts = 4 if lanes % (4 * LANES) == 0 else 1
     width = lanes // parts
-    size = len(message_rows(0, parts))
+    size = len(message_rows(parts))
     pairs = COILS * COILS
     vmem = pl.BlockSpec(memory_space=pltpu.VMEM)
     columns = jnp.transpose(kernels, (1, 2, 3, 0, 4)).reshape(TAP**3, 2, lanes)

time: 30.9 us -> 31 us (level)
  no operation moved by 1% of the time
where the time goes in v5:
time: 31 us; the launch traced here: 30.7 us
  Pallas kernels  30.6 us (99%)
    pallas_call x1, Pallas kernels, local(): pl.pallas_call(functools.partial(exchange_kernel, count, parts, width), o...  26.6 us
    pallas_call x1, Pallas kernels, local(): pl.pallas_call(depth_kernel, grid=(XD, 2), out_shape=jax.ShapeDtypeStruct...  4.04 us

profile of v5, /device:TPU:29, one launch (start us, length us, event | category | flops | bytes accessed | tf_op | source)
XLA Modules:
  0.0 30.7 jit_solution(9809477605769668111)
XLA Ops:
  0.0 26.6 %exchange.1.right = f32[2,32,1024]{2,1,0:T(8,128)} custom-call(bf16[216,2,1024]{2,1,0:T(2,128)(2,1)} %bitcast.3, bf16[2,256,864]{2,1,0:T(8,128)(2,1)} %constant.8.clone.planes, bf16[64,48]{1,0:T(8,128)(2,1)} %constant.9.clone.place, bf16[384,512]{1,0:T(8,128)(2,1)} %constant.10.clone.swap), custom_call_target="tpu_custom_call" | custom-call | tf_op jit(solution)/shard_map/exchange/pallas_call | solution.py:238
  26.6 4.0 %depth.1 = f32[2,2,1,192,1024]{4,3,2,1,0:T(8,128)} custom-call(f32[2,32,1024]{2,1,0:T(8,128)} %exchange.1.right, bf16[384,96]{1,0:T(8,128)(2,1)} %constant.11.clone.table), custom_call_target="tpu_custom_call" | custom-call | tf_op jit(solution)/shard_map/depth/pallas_call | solution.py:253
